TPU v7x, 128 devices: a whole 4x4x4 slice. The times are simulated.
128 devices in a mesh: dom: 128 (over y, x, z, core).
Axes of the slice: x: 4, y: 4, z: 4, core: 2. Of those that a mesh axis runs over, the one named last changes fastest.
Arguments:
- z_state: bfloat16 [96, 1048576], P(None, 'dom'), may hold values from 0 to 20, as said below
- inputs: bfloat16 [128, 1048576], P(None, 'dom'), may hold values from -6 to 6
- adjoint: bfloat16 [96, 1048576], P(None, 'dom'), may hold values from -6 to 6
- cotangent: bfloat16 [96, 1048576], P(None, 'dom'), may hold values from -0.59765625 to 0.59765625
- mix_weight: bfloat16 [96, 96], replicated, may hold values from -0.625 to 0.625
- input_weight: bfloat16 [96, 128], replicated, may hold values from -0.5 to 0.5
- tile_values: bfloat16 [32768, 128, 128], P('dom'), may hold values from 0 to 0.019897461
- tile_src: int32 [128, 256], P('dom'), may hold values from 0 to 191, as said below
- tile_dst: int32 [128, 256], P('dom'), may hold values from 0 to 63
- send_list: int32 [128, 8, 16], P('dom'), may hold values from 0 to 63
Outputs:
- fixed_next: bfloat16 [96, 1048576], P(None, 'dom')
- adjoint_next: bfloat16 [96, 1048576], P(None, 'dom')
- weight_grad: float32 [96, 96], replicated
- input_grad: float32 [96, 128], replicated
Inputs may be any that keep to these rules, and one draw needn't show every extreme that they name: `tile_src`: codes below 64 name a local tile; code 64 + o * 16 + c names slot c of neighbour o's list for this partition. Every code from 64 upward appears on every partition. `z_state`: zero or positive; a state after a rectifier.
All inputs are finite; a program needn't handle non-finite values.
Results may differ from a plain program's by a relative error of at most 0.0058.
Values may be sent and summed in bfloat16 or wider, within the bound.
No kernel may reach another device: no remote copies, remote signals or barrier semaphores. Data moves between devices by JAX's collectives and lax.ppermute only.
A program may use at most 128 MiB of HBM per device.

v0:
```python
import math

import jax
import jax.numpy as jnp
from jax import lax
from jax.experimental import pallas as pl
from jax.experimental.pallas import tpu as pltpu
from jax.sharding import PartitionSpec as P


AXIS = "dom"
H = 96
F = 128
T = 128
LOC = 64
CAP = 16
PEERS = 8
TILES = 256
NODES_DEV = LOC * T
CODES = LOC + PEERS * CAP
CHUNKS = 8
PER = TILES // CHUNKS
UNROLL = 8
OFFSETS = (1, 2, 3, 4, -1, -2, -3, -4)
ORDER = (7, 3, 6, 2, 5, 1, 4, 0)
BF = jnp.bfloat16
F32 = jnp.float32


ANY = pl.BlockSpec(memory_space=pl.ANY)
SMEM = pl.BlockSpec(memory_space=pltpu.SMEM)
VMEM = pl.BlockSpec(memory_space=pltpu.VMEM)


def params(mib):
    return pltpu.CompilerParams(vmem_limit_bytes=mib * 1024 * 1024)


def cols(t, width=T):
    return pl.ds(pl.multiple_of(t * width, width), width)


def gather_body(send, z, *outs):
    for o in ORDER:
        for c in range(CAP):
            outs[o][c] = z[:, cols(send[o, c])]


def gather_lists(send_ids, z_state):
    return pl.pallas_call(
        gather_body,
        name="gather_lists",
        out_shape=[jax.ShapeDtypeStruct((CAP, H, T), BF)] * PEERS,
        in_specs=[SMEM, VMEM],
        out_specs=[VMEM] * PEERS,
        compiler_params=params(16),
        cost_estimate=pl.CostEstimate(flops=10**9, transcendentals=0, bytes_accessed=5 * 2**20),
    )(send_ids, z_state)


def tile_copies(v_hbm, v, sems):
    return [
        pltpu.make_async_copy(
            v_hbm.at[pl.ds(i * PER, PER)], v.at[pl.ds(i * PER, PER)], sems.at[i]
        )
        for i in range(CHUNKS)
    ]


def back_body(src, dst, z_hbm, adj_hbm, cot_hbm, w, v_hbm, *rest):
    outs = rest[:PEERS]
    base_hbm, masked_hbm = rest[PEERS : PEERS + 2]
    z, masked, cot, v, back, acc, packed, sems, v_sems, out_sems = rest[PEERS + 2 :]
    load_z = pltpu.make_async_copy(z_hbm, z, sems.at[0])
    load_a = pltpu.make_async_copy(adj_hbm, masked, sems.at[1])
    load_c = pltpu.make_async_copy(cot_hbm, cot, sems.at[2])
    load_v = tile_copies(v_hbm, v, v_sems)
    load_z.start()
    load_a.start()
    load_c.start()
    for copy in load_v:
        copy.start()

    def clear(j, carry):
        acc[LOC + j] = jnp.zeros((H, T), F32)
        return carry

    lax.fori_loop(0, PEERS * CAP, clear, 0, unroll=4)
    load_z.wait()
    load_a.wait()
    wt = w[...]

    def mask(i, carry):
        at = cols(i, 4 * T)
        kept = jnp.where(z[:, at].astype(F32) > 0, masked[:, at].astype(F32), 0.0).astype(BF)
        masked[:, at] = kept
        moved = lax.dot_general(wt, kept, (((0,), (0,)), ((), ())), preferred_element_type=F32)
        moved = moved.astype(BF)
        for j in range(4):
            back[i * 4 + j] = moved[:, j * T : (j + 1) * T]
        return carry

    lax.fori_loop(0, LOC // 4, mask, 0)
    keep = pltpu.make_async_copy(masked, masked_hbm, sems.at[3])
    keep.start()
    load_c.wait()

    def start(t, carry):
        acc[t] = cot[:, cols(t)].astype(F32)
        return carry

    lax.fori_loop(0, LOC, start, 0, unroll=4)
    for i in range(CHUNKS):
        load_v[i].wait()

        def step(g, carry):
            first = i * PER + g * UNROLL
            parts = [
                lax.dot_general(
                    back[dst[first + u]],
                    v[first + u],
                    (((1,), (1,)), ((), ())),
                    preferred_element_type=F32,
                )
                for u in range(UNROLL)
            ]
            for u in range(UNROLL):
                s = src[first + u]
                acc[s] = acc[s] + parts[u]
            return carry

        lax.fori_loop(0, PER // UNROLL, step, 0)
    copies = []
    for n, o in enumerate(ORDER):

        def pack(c, carry):
            packed[o * CAP + c] = acc[LOC + o * CAP + c].astype(BF)
            return carry

        lax.fori_loop(0, CAP, pack, 0, unroll=4)
        copy = pltpu.make_async_copy(packed.at[pl.ds(o * CAP, CAP)], outs[o], out_sems.at[n])
        copy.start()
        copies.append(copy)
    base = pltpu.make_async_copy(acc.at[pl.ds(0, LOC)], base_hbm, sems.at[4])
    base.start()
    for copy in copies:
        copy.wait()
    base.wait()
    keep.wait()


def back_partials(src, dst, z_state, adjoint, cotangent, mix_weight, tile_values):
    outs = pl.pallas_call(
        back_body,
        name="back_partials",
        out_shape=[jax.ShapeDtypeStruct((CAP, H, T), BF)] * PEERS
        + [
            jax.ShapeDtypeStruct((LOC, H, T), F32),
            jax.ShapeDtypeStruct((H, NODES_DEV), BF),
        ],
        in_specs=[SMEM, SMEM, ANY, ANY, ANY, VMEM, ANY],
        out_specs=[ANY] * (PEERS + 2),
        scratch_shapes=[
            pltpu.VMEM((H, NODES_DEV), BF),
            pltpu.VMEM((H, NODES_DEV), BF),
            pltpu.VMEM((H, NODES_DEV), BF),
            pltpu.VMEM((TILES, T, T), BF),
            pltpu.VMEM((LOC, H, T), BF),
            pltpu.VMEM((CODES, H, T), F32),
            pltpu.VMEM((PEERS * CAP, H, T), BF),
            pltpu.SemaphoreType.DMA((5,)),
            pltpu.SemaphoreType.DMA((CHUNKS,)),
            pltpu.SemaphoreType.DMA((PEERS,)),
        ],
        compiler_params=params(44),
        cost_estimate=pl.CostEstimate(
            flops=4 * 10**9, transcendentals=0, bytes_accessed=20 * 2**20
        ),
    )(src, dst, z_state, adjoint, cotangent, mix_weight, tile_values)
    return outs[:PEERS], outs[PEERS], outs[PEERS + 1]


def input_body(masked, inputs, out):
    total = jnp.zeros((H, F), F32)
    width = 8 * T

    def step(i, total):
        at = cols(i, width)
        return total + lax.dot_general(
            masked[:, at], inputs[:, at], (((1,), (1,)), ((), ())), preferred_element_type=F32
        )

    out[...] = lax.fori_loop(0, NODES_DEV // width, step, total)


def input_product(masked, inputs):
    return pl.pallas_call(
        input_body,
        name="input_product",
        out_shape=jax.ShapeDtypeStruct((H, F), F32),
        in_specs=[VMEM, VMEM],
        out_specs=VMEM,
        compiler_params=params(16),
        cost_estimate=pl.CostEstimate(
            flops=10**9, transcendentals=0, bytes_accessed=4 * 2**20
        ),
    )(masked, inputs)


def forward_body(src, dst, z_hbm, x_hbm, m_hbm, w, b, v_hbm, grad, *rest):
    arrived = rest[:PEERS]
    next_hbm, red = rest[PEERS : PEERS + 2]
    z, x, m, v, table, agg, sems, v_sems, in_sems = rest[PEERS + 2 :]
    load_z = pltpu.make_async_copy(z_hbm, z, sems.at[0])
    load_x = pltpu.make_async_copy(x_hbm, x, sems.at[1])
    load_m = pltpu.make_async_copy(m_hbm, m, sems.at[2])
    load_v = tile_copies(v_hbm, v, v_sems)
    halo = [
        pltpu.make_async_copy(
            arrived[o], table.at[pl.ds(LOC + o * CAP, CAP)], in_sems.at[o]
        )
        for o in range(PEERS)
    ]
    load_z.start()
    for copy in halo:
        copy.start()
    for copy in load_v:
        copy.start()
    load_x.start()
    load_m.start()

    def clear(t, carry):
        agg[t] = jnp.zeros((H, T), F32)
        return carry

    lax.fori_loop(0, LOC, clear, 0, unroll=4)
    load_z.wait()

    def local(t, carry):
        table[t] = z[:, cols(t)]
        return carry

    lax.fori_loop(0, LOC, local, 0, unroll=4)
    for copy in halo:
        copy.wait()
    for i in range(CHUNKS):
        load_v[i].wait()

        def step(g, carry):
            first = i * PER + g * UNROLL
            parts = [
                jnp.dot(table[src[first + u]], v[first + u], preferred_element_type=F32)
                for u in range(UNROLL)
            ]
            for u in range(UNROLL):
                d = dst[first + u]
                agg[d] = agg[d] + parts[u]
            return carry

        lax.fori_loop(0, PER // UNROLL, step, 0)
    load_x.wait()
    load_m.wait()
    wt = w[...]
    bt = b[...]

    def finish(i, total):
        at = cols(i, 4 * T)
        a = jnp.concatenate([agg[i * 4 + j].astype(BF) for j in range(4)], axis=1)
        pre = jnp.dot(wt, a, preferred_element_type=F32) + jnp.dot(
            bt, x[:, at], preferred_element_type=F32
        )
        z[:, at] = jnp.maximum(pre, 0.0).astype(BF)
        return total + lax.dot_general(
            m[:, at], a, (((1,), (1,)), ((), ())), preferred_element_type=F32
        )

    total = lax.fori_loop(0, LOC // 4, finish, jnp.zeros((H, H), F32))
    store = pltpu.make_async_copy(z, next_hbm, sems.at[0])
    store.start()
    scale = 1.0 / math.sqrt(NODES_DEV * 128)
    red[:, :F] = grad[...] * scale
    red[:, F : F + H] = total * scale
    red[:, F + H :] = jnp.zeros((H, 2 * T - F - H), F32)
    store.wait()


def forward(src, dst, z_state, inputs, masked, mix_weight, input_weight, tile_values, grad, lists):
    return pl.pallas_call(
        forward_body,
        name="forward",
        out_shape=[
            jax.ShapeDtypeStruct((H, NODES_DEV), BF),
            jax.ShapeDtypeStruct((H, 2 * T), F32),
        ],
        in_specs=[SMEM, SMEM, ANY, ANY, ANY, VMEM, VMEM, ANY, VMEM] + [ANY] * PEERS,
        out_specs=[ANY, VMEM],
        scratch_shapes=[
            pltpu.VMEM((H, NODES_DEV), BF),
            pltpu.VMEM((F, NODES_DEV), BF),
            pltpu.VMEM((H, NODES_DEV), BF),
            pltpu.VMEM((TILES, T, T), BF),
            pltpu.VMEM((CODES, H, T), BF),
            pltpu.VMEM((LOC, H, T), F32),
            pltpu.SemaphoreType.DMA((3,)),
            pltpu.SemaphoreType.DMA((CHUNKS,)),
            pltpu.SemaphoreType.DMA((PEERS,)),
        ],
        compiler_params=params(44),
        cost_estimate=pl.CostEstimate(
            flops=4 * 10**9, transcendentals=0, bytes_accessed=20 * 2**20
        ),
    )(src, dst, z_state, inputs, masked, mix_weight, input_weight, tile_values, grad, *lists)


def finish_body(send, base_hbm, *rest):
    lists = rest[:PEERS]
    out = rest[PEERS]
    acc, parts, sem, in_sems = rest[PEERS + 1 :]
    load = pltpu.make_async_copy(base_hbm, acc, sem.at[0])
    load.start()
    copies = [
        pltpu.make_async_copy(lists[o], parts.at[pl.ds(o * CAP, CAP)], in_sems.at[o])
        for o in range(PEERS)
    ]
    for copy in copies:
        copy.start()
    load.wait()
    for o in range(PEERS):
        copies[o].wait()
        for c in range(CAP):
            t = send[o, c]
            acc[t] = acc[t] + parts[o * CAP + c].astype(F32)
    for t in range(LOC):
        out[:, t * T : (t + 1) * T] = acc[t].astype(BF)


def finish_adjoint(send_ids, base, lists):
    return pl.pallas_call(
        finish_body,
        name="finish_adjoint",
        out_shape=jax.ShapeDtypeStruct((H, NODES_DEV), BF),
        in_specs=[SMEM, ANY] + [ANY] * PEERS,
        out_specs=VMEM,
        scratch_shapes=[
            pltpu.VMEM((LOC, H, T), F32),
            pltpu.VMEM((PEERS * CAP, H, T), BF),
            pltpu.SemaphoreType.DMA((1,)),
            pltpu.SemaphoreType.DMA((PEERS,)),
        ],
        compiler_params=params(24),
        cost_estimate=pl.CostEstimate(
            flops=10**9, transcendentals=0, bytes_accessed=8 * 2**20
        ),
    )(send_ids, base, *lists)


def shift(array, by):
    n = lax.axis_size(AXIS)
    return lax.ppermute(array, AXIS, [(i, (i + by) % n) for i in range(n)])


def swap(array, bits):
    n = lax.axis_size(AXIS)
    return lax.ppermute(array, AXIS, [(i, i ^ bits) for i in range(n)])


def summed(total):
    for low in (5, 3, 1):
        one, two, three = (swap(total, k << low) for k in (1, 2, 3))
        total = (total + one) + (two + three)
    return total + swap(total, 1)


def exchange(lists, sign):
    got = [None] * PEERS
    for o in ORDER:
        got[o] = shift(lists[o], sign * OFFSETS[o])
    return got


def per_device(
    z_state,
    inputs,
    adjoint,
    cotangent,
    mix_weight,
    input_weight,
    tile_values,
    tile_src,
    tile_dst,
    send_list,
):
    src, dst, send_ids = tile_src[0], tile_dst[0], send_list[0]
    arrived = exchange(gather_lists(send_ids, z_state), 1)
    leaving, base, masked = back_partials(
        src, dst, z_state, adjoint, cotangent, mix_weight, tile_values
    )
    returned = exchange(leaving, -1)
    grad = input_product(masked, inputs)
    fixed_next, red = forward(
        src, dst, z_state, inputs, masked, mix_weight, input_weight, tile_values, grad,
        arrived,
    )
    total = summed(red)
    adjoint_next = finish_adjoint(send_ids, base, returned)
    return fixed_next, adjoint_next, total[:, F : F + H], total[:, :F]


def solution(mesh):
    dom = P(None, AXIS)
    return jax.shard_map(
        per_device,
        mesh=mesh,
        in_specs=(
            dom,
            dom,
            dom,
            dom,
            P(),
            P(),
            P(AXIS, None, None),
            P(AXIS, None),
            P(AXIS, None),
            P(AXIS, None, None),
        ),
        out_specs=(dom, dom, P(), P()),
        check_vma=False,
    )
```

profile of v0, /device:TPU:40, one launch (start us, length us, event | category | flops | bytes accessed | tf_op | source)
XLA Modules:
  0.0 178.0 jit_solution(10603544509904242856)
XLA Ops:
  0.6 1.4 copy-done.2
  2.7 1.4 gather_lists.1
  4.3 2.0 %collective-permute-start.1 = (bf16[16,96,128]{2,1,0:T(8,128)(2,1)S(1)}, bf16[16,96,128]{2,1,0:T(8,128)(2,1)S(1)}, u32[]{:S(2)}, u32[]{:S(2)}) collective-permute-start(bf16[16,96,128]{2,1,0:T(8,128)(2,1)S(1)} %get-tuple-element.26), channel_id=1, source_target_pairs={{0,2},{1,3},{2,4},{3,5},{4,6},{5,7},{6,8},{7,9},{8,10},{9,11},{10,... | collective-permute-start | bytes 1179656 | tf_op jit(solution)/shard_map/ppermute | solution.py:359
  6.2 1.3 collective-permute-start.2
  7.5 3.1 %collective-permute-start.3 = (bf16[16,96,128]{2,1,0:T(8,128)(2,1)S(1)}, bf16[16,96,128]{2,1,0:T(8,128)(2,1)S(1)}, u32[]{:S(2)}, u32[]{:S(2)}) collective-permute-start(bf16[16,96,128]{2,1,0:T(8,128)(2,1)S(1)} %get-tuple-element.28), channel_id=1, source_target_pairs={{0,4},{1,5},{2,6},{3,7},{4,8},{5,9},{6,10},{7,11},{8,12},{9,13},{1... | collective-permute-start | bytes 1179656 | tf_op jit(solution)/shard_map/ppermute | solution.py:359
  10.6 4.4 %collective-permute-done.rest_0_ = bf16[16,96,128]{2,1,0:T(8,128)(2,1)S(1)} collective-permute-done((bf16[16,96,128]{2,1,0:T(8,128)(2,1)S(1)}, bf16[16,96,128]{2,1,0:T(8,128)(2,1)S(1)}, u32[]{:S(2)}, u32[]{:S(2)}) %collective-permute-start) | collective-permute-done | bytes 393248 | tf_op jit(solution)/shard_map/ppermute | solution.py:359
  15.0 10.2 %collective-permute-start.5 = (bf16[16,96,128]{2,1,0:T(8,128)(2,1)S(1)}, bf16[16,96,128]{2,1,0:T(8,128)(2,1)S(1)}, u32[]{:S(2)}, u32[]{:S(2)}) collective-permute-start(bf16[16,96,128]{2,1,0:T(8,128)(2,1)S(1)} %get-tuple-element.30), channel_id=1, source_target_pairs={{0,126},{1,127},{2,0},{3,1},{4,2},{5,3},{6,4},{7,5},{8,6},{9,7},{1... | collective-permute-start | bytes 1179656 | tf_op jit(solution)/shard_map/ppermute | solution.py:359
  25.2 15.7 %collective-permute-start.6 = (bf16[16,96,128]{2,1,0:T(8,128)(2,1)S(1)}, bf16[16,96,128]{2,1,0:T(8,128)(2,1)S(1)}, u32[]{:S(2)}, u32[]{:S(2)}) collective-permute-start(bf16[16,96,128]{2,1,0:T(8,128)(2,1)S(1)} %get-tuple-element.31), channel_id=1, source_target_pairs={{0,125},{1,126},{2,127},{3,0},{4,1},{5,2},{6,3},{7,4},{8,5},{9,6},... | collective-permute-start | bytes 1179656 | tf_op jit(solution)/shard_map/ppermute | solution.py:359
  40.8 6.9 %collective-permute-done.2.rest_2_ = bf16[16,96,128]{2,1,0:T(8,128)(2,1)S(1)} collective-permute-done((bf16[16,96,128]{2,1,0:T(8,128)(2,1)S(1)}, bf16[16,96,128]{2,1,0:T(8,128)(2,1)S(1)}, u32[]{:S(2)}, u32[]{:S(2)}) %collective-permute-start.2) | collective-permute-done | bytes 393248 | tf_op jit(solution)/shard_map/ppermute | solution.py:359
  47.8 1.4 copy-done.11
  49.2 18.4 %back_partials.1 = (bf16[16,96,128]{2,1,0:T(8,128)(2,1)S(1)}, bf16[16,96,128]{2,1,0:T(8,128)(2,1)S(1)}, bf16[16,96,128]{2,1,0:T(8,128)(2,1)S(1)}, bf16[16,96,128...) custom-call(s32[256]{0:T(256)S(1)} %bitcast.5, ...), custom_call_target="tpu_custom_call" | custom-call | flops 4000000000 | bytes 20971520 | tf_op jit(solution)/shard_map/back_partials/pallas_call | solution.py:153
  67.6 1.8 input_product.1.grad
  69.4 15.4 %forward.1 = (bf16[96,8192]{1,0:T(8,128)(2,1)}, f32[96,256]{1,0:T(8,128)S(1)}) custom-call(s32[256]{0:T(256)S(1)} %bitcast.6, s32[256]{0:T(256)S(1)} %bitcast.8, bf16[96,8192]{1,0:T(8,128)(2,1)S(1)} %copy-done.3, bf16[128,8192]{1,0:T(8,128)(2,1)S(1)} %copy-done, bf16[96,8192]{1,0:T(8,128)(2,1)S(1)} %get-tuple-element.24.masked.m_hbm, ...), custom_call_target="tpu_custom_call" | custom-call | flops 4000000000 | bytes 20971520 | tf_op jit(solution)/shard_map/forward/pallas_call | solution.py:288
  84.9 1.6 collective-permute-start.18
  86.5 1.6 collective-permute-start.17
  88.1 1.0 collective-permute-start.16
  89.6 3.1 %collective-permute-done.17 = f32[96,256]{1,0:T(8,128)S(1)} collective-permute-done((f32[96,256]{1,0:T(8,128)S(1)}, f32[96,256]{1,0:T(8,128)S(1)}, u32[]{:S(2)}, u32[]{:S(2)}) %collective-permute-start.17) | collective-permute-done | bytes 98336 | tf_op jit(solution)/shard_map/ppermute | solution.py:364
  94.4 2.5 %collective-permute-start.19 = (f32[96,256]{1,0:T(8,128)S(1)}, f32[96,256]{1,0:T(8,128)S(1)}, u32[]{:S(2)}, u32[]{:S(2)}) collective-permute-start(f32[96,256]{1,0:T(8,128)S(1)} %add_add_fusion.2), channel_id=1, source_target_pairs={{0,8},{1,9},{2,10},{3,11},{4,12},{5,13},{6,14},{7,15},{8,0},{9,1},... | collective-permute-start | bytes 294920 | tf_op jit(solution)/shard_map/ppermute | solution.py:364
  97.0 3.8 %collective-permute-done.21 = f32[96,256]{1,0:T(8,128)S(1)} collective-permute-done((f32[96,256]{1,0:T(8,128)S(1)}, f32[96,256]{1,0:T(8,128)S(1)}, u32[]{:S(2)}, u32[]{:S(2)}) %collective-permute-start.21) | collective-permute-done | bytes 98336 | tf_op jit(solution)/shard_map/ppermute | solution.py:364
  101.2 1.0 collective-permute-done.19
  102.3 1.4 collective-permute-start.24
  103.7 2.2 %collective-permute-start.23 = (f32[96,256]{1,0:T(8,128)S(1)}, f32[96,256]{1,0:T(8,128)S(1)}, u32[]{:S(2)}, u32[]{:S(2)}) collective-permute-start(f32[96,256]{1,0:T(8,128)S(1)} %add_add_fusion.1), channel_id=1, source_target_pairs={{0,4},{1,5},{2,6},{3,7},{4,0},{5,1},{6,2},{7,3},{8,12},{9,13},{10,... | collective-permute-start | bytes 294920 | tf_op jit(solution)/shard_map/ppermute | solution.py:364
  105.9 1.1 collective-permute-start.22
  107.0 6.0 %collective-permute-done.9.rest_1_ = bf16[16,96,128]{2,1,0:T(8,128)(2,1)S(1)} collective-permute-done((bf16[16,96,128]{2,1,0:T(8,128)(2,1)S(1)}, bf16[16,96,128]{2,1,0:T(8,128)(2,1)S(1)}, u32[]{:S(2)}, u32[]{:S(2)}) %collective-permute-start.9) | collective-permute-done | bytes 393248 | tf_op jit(solution)/shard_map/ppermute | solution.py:359
  113.0 9.3 %collective-permute-start.11 = (bf16[16,96,128]{2,1,0:T(8,128)(2,1)S(1)}, bf16[16,96,128]{2,1,0:T(8,128)(2,1)S(1)}, u32[]{:S(2)}, u32[]{:S(2)}) collective-permute-start(bf16[16,96,128]{2,1,0:T(8,128)(2,1)S(1)} %get-tuple-element.38), channel_id=1, source_target_pairs={{0,124},{1,125},{2,126},{3,127},{4,0},{5,1},{6,2},{7,3},{8,4},{9,5... | collective-permute-start | bytes 1179656 | tf_op jit(solution)/shard_map/ppermute | solution.py:359
  122.3 4.7 %collective-permute-start.13 = (bf16[16,96,128]{2,1,0:T(8,128)(2,1)S(1)}, bf16[16,96,128]{2,1,0:T(8,128)(2,1)S(1)}, u32[]{:S(2)}, u32[]{:S(2)}) collective-permute-start(bf16[16,96,128]{2,1,0:T(8,128)(2,1)S(1)} %get-tuple-element.40), channel_id=1, source_target_pairs={{0,2},{1,3},{2,4},{3,5},{4,6},{5,7},{6,8},{7,9},{8,10},{9,11},{10,... | collective-permute-start | bytes 1179656 | tf_op jit(solution)/shard_map/ppermute | solution.py:359
  127.0 7.5 %collective-permute-start.14 = (bf16[16,96,128]{2,1,0:T(8,128)(2,1)S(1)}, bf16[16,96,128]{2,1,0:T(8,128)(2,1)S(1)}, u32[]{:S(2)}, u32[]{:S(2)}) collective-permute-start(bf16[16,96,128]{2,1,0:T(8,128)(2,1)S(1)} %get-tuple-element.41), channel_id=1, source_target_pairs={{0,3},{1,4},{2,5},{3,6},{4,7},{5,8},{6,9},{7,10},{8,11},{9,12},{10... | collective-permute-start | bytes 1179656 | tf_op jit(solution)/shard_map/ppermute | solution.py:359
  134.8 6.0 %collective-permute-done.12.rest_4_ = bf16[16,96,128]{2,1,0:T(8,128)(2,1)S(1)} collective-permute-done((bf16[16,96,128]{2,1,0:T(8,128)(2,1)S(1)}, bf16[16,96,128]{2,1,0:T(8,128)(2,1)S(1)}, u32[]{:S(2)}, u32[]{:S(2)}) %collective-permute-start.12) | collective-permute-done | bytes 393248 | tf_op jit(solution)/shard_map/ppermute | solution.py:359
  140.9 1.2 collective-permute-done.13.rest_5_
  142.0 20.8 %collective-permute-done.14.rest_6_ = bf16[16,96,128]{2,1,0:T(8,128)(2,1)S(1)} collective-permute-done((bf16[16,96,128]{2,1,0:T(8,128)(2,1)S(1)}, bf16[16,96,128]{2,1,0:T(8,128)(2,1)S(1)}, u32[]{:S(2)}, u32[]{:S(2)}) %collective-permute-start.14) | collective-permute-done | bytes 393248 | tf_op jit(solution)/shard_map/ppermute | solution.py:359
  162.8 9.3 %collective-permute-done.15.rest_7_ = bf16[16,96,128]{2,1,0:T(8,128)(2,1)S(1)} collective-permute-done((bf16[16,96,128]{2,1,0:T(8,128)(2,1)S(1)}, bf16[16,96,128]{2,1,0:T(8,128)(2,1)S(1)}, u32[]{:S(2)}, u32[]{:S(2)}) %collective-permute-start.15) | collective-permute-done | bytes 393248 | tf_op jit(solution)/shard_map/ppermute | solution.py:359
  172.1 4.6 %finish_adjoint.1 = bf16[96,8192]{1,0:T(8,128)(2,1)} custom-call(s32[8,16]{1,0:T(8,128)S(1)} %bitcast.4, f32[64,96,128]{2,1,0:T(8,128)S(1)} %copy-done.1, bf16[16,96,128]{2,1,0:T(8,128)(2,1)S(1)} %collective-permute-done.8.rest_0_, bf16[16,96,128]{2,1,0:T(8,128)(2,1)S(1)} %collective-permute-done.9.rest_1_, ...), custom_call_target="tpu_custom_call" | custom-call | flops 1000000000 | bytes 8388608 | tf_op jit(solution)/shard_map/finish_adjoint/pallas_call | solution.py:338
  (55 shorter events, 5.2 us)
Async XLA Ops:
  2.7 45.0 %copy-start.4 = (bf16[96,96]{1,0:T(8,128)(2,1)S(1)}, bf16[96,96]{1,0:T(8,128)(2,1)}, u32[]{:S(2)}) copy-start(bf16[96,96]{1,0:T(8,128)(2,1)} %w.3) | copy-start | bytes 55300
  2.7 45.0 %copy-start.8 = (s32[1,256]{1,0:T(1,128)S(1)}, s32[1,256]{1,0:T(1,128)}, u32[]{:S(2)}) copy-start(s32[1,256]{1,0:T(1,128)} %param.17) | copy-start | bytes 3076
  2.7 45.0 %copy-start.9 = (s32[1,256]{1,0:T(1,128)S(1)}, s32[1,256]{1,0:T(1,128)}, u32[]{:S(2)}) copy-start(s32[1,256]{1,0:T(1,128)} %param.18) | copy-start | bytes 3076
  2.7 45.0 %copy-start.10 = (bf16[96,8192]{1,0:T(8,128)(2,1)S(1)}, bf16[96,8192]{1,0:T(8,128)(2,1)}, u32[]{:S(2)}) copy-start(bf16[96,8192]{1,0:T(8,128)(2,1)} %adj_hbm.1) | copy-start | bytes 4718596
  4.2 10.8 %collective-permute-start = (bf16[16,96,128]{2,1,0:T(8,128)(2,1)S(1)}, bf16[16,96,128]{2,1,0:T(8,128)(2,1)S(1)}, u32[]{:S(2)}, u32[]{:S(2)}) collective-permute-start(bf16[16,96,128]{2,1,0:T(8,128)(2,1)S(1)} %get-tuple-element.25), channel_id=1, source_target_pairs={{0,1},{1,2},{2,3},{3,4},{4,5},{5,6},{6,7},{7,8},{8,9},{9,10},{10,1... | collective-permute-start | bytes 1179656 | tf_op jit(solution)/shard_map/ppermute | solution.py:359
  4.3 20.9 %collective-permute-start.1 = (bf16[16,96,128]{2,1,0:T(8,128)(2,1)S(1)}, bf16[16,96,128]{2,1,0:T(8,128)(2,1)S(1)}, u32[]{:S(2)}, u32[]{:S(2)}) collective-permute-start(bf16[16,96,128]{2,1,0:T(8,128)(2,1)S(1)} %get-tuple-element.26), channel_id=1, source_target_pairs={{0,2},{1,3},{2,4},{3,5},{4,6},{5,7},{6,8},{7,9},{8,10},{9,11},{10,... | collective-permute-start | bytes 1179656 | tf_op jit(solution)/shard_map/ppermute | solution.py:359
  6.2 41.5 %collective-permute-start.2 = (bf16[16,96,128]{2,1,0:T(8,128)(2,1)S(1)}, bf16[16,96,128]{2,1,0:T(8,128)(2,1)S(1)}, u32[]{:S(2)}, u32[]{:S(2)}) collective-permute-start(bf16[16,96,128]{2,1,0:T(8,128)(2,1)S(1)} %get-tuple-element.27), channel_id=1, source_target_pairs={{0,3},{1,4},{2,5},{3,6},{4,7},{5,8},{6,9},{7,10},{8,11},{9,12},{10... | collective-permute-start | bytes 1179656 | tf_op jit(solution)/shard_map/ppermute | solution.py:359
  7.5 61.9 %collective-permute-start.3 = (bf16[16,96,128]{2,1,0:T(8,128)(2,1)S(1)}, bf16[16,96,128]{2,1,0:T(8,128)(2,1)S(1)}, u32[]{:S(2)}, u32[]{:S(2)}) collective-permute-start(bf16[16,96,128]{2,1,0:T(8,128)(2,1)S(1)} %get-tuple-element.28), channel_id=1, source_target_pairs={{0,4},{1,5},{2,6},{3,7},{4,8},{5,9},{6,10},{7,11},{8,12},{9,13},{1... | collective-permute-start | bytes 1179656 | tf_op jit(solution)/shard_map/ppermute | solution.py:359
  10.6 58.7 %collective-permute-start.4 = (bf16[16,96,128]{2,1,0:T(8,128)(2,1)S(1)}, bf16[16,96,128]{2,1,0:T(8,128)(2,1)S(1)}, u32[]{:S(2)}, u32[]{:S(2)}) collective-permute-start(bf16[16,96,128]{2,1,0:T(8,128)(2,1)S(1)} %get-tuple-element.29), channel_id=1, source_target_pairs={{0,127},{1,0},{2,1},{3,2},{4,3},{5,4},{6,5},{7,6},{8,7},{9,8},{10,... | collective-permute-start | bytes 1179656 | tf_op jit(solution)/shard_map/ppermute | solution.py:359
  15.0 54.4 %collective-permute-start.5 = (bf16[16,96,128]{2,1,0:T(8,128)(2,1)S(1)}, bf16[16,96,128]{2,1,0:T(8,128)(2,1)S(1)}, u32[]{:S(2)}, u32[]{:S(2)}) collective-permute-start(bf16[16,96,128]{2,1,0:T(8,128)(2,1)S(1)} %get-tuple-element.30), channel_id=1, source_target_pairs={{0,126},{1,127},{2,0},{3,1},{4,2},{5,3},{6,4},{7,5},{8,6},{9,7},{1... | collective-permute-start | bytes 1179656 | tf_op jit(solution)/shard_map/ppermute | solution.py:359
  25.2 44.2 %collective-permute-start.6 = (bf16[16,96,128]{2,1,0:T(8,128)(2,1)S(1)}, bf16[16,96,128]{2,1,0:T(8,128)(2,1)S(1)}, u32[]{:S(2)}, u32[]{:S(2)}) collective-permute-start(bf16[16,96,128]{2,1,0:T(8,128)(2,1)S(1)} %get-tuple-element.31), channel_id=1, source_target_pairs={{0,125},{1,126},{2,127},{3,0},{4,1},{5,2},{6,3},{7,4},{8,5},{9,6},... | collective-permute-start | bytes 1179656 | tf_op jit(solution)/shard_map/ppermute | solution.py:359
  47.7 21.7 %collective-permute-start.7 = (bf16[16,96,128]{2,1,0:T(8,128)(2,1)S(1)}, bf16[16,96,128]{2,1,0:T(8,128)(2,1)S(1)}, u32[]{:S(2)}, u32[]{:S(2)}) collective-permute-start(bf16[16,96,128]{2,1,0:T(8,128)(2,1)S(1)} %get-tuple-element.32), channel_id=1, source_target_pairs={{0,124},{1,125},{2,126},{3,127},{4,0},{5,1},{6,2},{7,3},{8,4},{9,5... | collective-permute-start | bytes 1179656 | tf_op jit(solution)/shard_map/ppermute | solution.py:359
  69.3 102.7 %copy-start.7 = (s32[1,8,16]{2,1,0:T(8,128)S(1)}, s32[1,8,16]{2,1,0:T(8,128)}, u32[]{:S(2)}) copy-start(s32[1,8,16]{2,1,0:T(8,128)} %param.19) | copy-start | bytes 1540
  69.4 102.7 %copy-start.1 = (f32[64,96,128]{2,1,0:T(8,128)S(1)}, f32[64,96,128]{2,1,0:T(8,128)}, u32[]{:S(2)}) copy-start(f32[64,96,128]{2,1,0:T(8,128)} %get-tuple-element.34.base_hbm) | copy-start | bytes 9437188
  84.9 4.8 %collective-permute-start.18 = (f32[96,256]{1,0:T(8,128)S(1)}, f32[96,256]{1,0:T(8,128)S(1)}, u32[]{:S(2)}, u32[]{:S(2)}) collective-permute-start(f32[96,256]{1,0:T(8,128)S(1)} %get-tuple-element.43), channel_id=1, source_target_pairs={{0,96},{1,97},{2,98},{3,99},{4,100},{5,101},{6,102},{7,103},{8,104... | collective-permute-start | bytes 294920 | tf_op jit(solution)/shard_map/ppermute | solution.py:364
  86.5 6.3 %collective-permute-start.17 = (f32[96,256]{1,0:T(8,128)S(1)}, f32[96,256]{1,0:T(8,128)S(1)}, u32[]{:S(2)}, u32[]{:S(2)}) collective-permute-start(f32[96,256]{1,0:T(8,128)S(1)} %get-tuple-element.43), channel_id=1, source_target_pairs={{0,64},{1,65},{2,66},{3,67},{4,68},{5,69},{6,70},{7,71},{8,72},{9,... | collective-permute-start | bytes 294920 | tf_op jit(solution)/shard_map/ppermute | solution.py:364
  88.1 4.7 %collective-permute-start.16 = (f32[96,256]{1,0:T(8,128)S(1)}, f32[96,256]{1,0:T(8,128)S(1)}, u32[]{:S(2)}, u32[]{:S(2)}) collective-permute-start(f32[96,256]{1,0:T(8,128)S(1)} %get-tuple-element.43), channel_id=1, source_target_pairs={{0,32},{1,33},{2,34},{3,35},{4,36},{5,37},{6,38},{7,39},{8,40},{9,... | collective-permute-start | bytes 294920 | tf_op jit(solution)/shard_map/ppermute | solution.py:364
  92.8 8.0 %collective-permute-start.21 = (f32[96,256]{1,0:T(8,128)S(1)}, f32[96,256]{1,0:T(8,128)S(1)}, u32[]{:S(2)}, u32[]{:S(2)}) collective-permute-start(f32[96,256]{1,0:T(8,128)S(1)} %add_add_fusion.2), channel_id=1, source_target_pairs={{0,24},{1,25},{2,26},{3,27},{4,28},{5,29},{6,30},{7,31},{8,16},{9,... | collective-permute-start | bytes 294920 | tf_op jit(solution)/shard_map/ppermute | solution.py:364
  93.5 12.4 %collective-permute-start.8 = (bf16[16,96,128]{2,1,0:T(8,128)(2,1)S(1)}, bf16[16,96,128]{2,1,0:T(8,128)(2,1)S(1)}, u32[]{:S(2)}, u32[]{:S(2)}) collective-permute-start(bf16[16,96,128]{2,1,0:T(8,128)(2,1)S(1)} %get-tuple-element.35), channel_id=1, source_target_pairs={{0,127},{1,0},{2,1},{3,2},{4,3},{5,4},{6,5},{7,6},{8,7},{9,8},{10,... | collective-permute-start | bytes 1179656 | tf_op jit(solution)/shard_map/ppermute | solution.py:359
  93.5 7.7 %collective-permute-start.20 = (f32[96,256]{1,0:T(8,128)S(1)}, f32[96,256]{1,0:T(8,128)S(1)}, u32[]{:S(2)}, u32[]{:S(2)}) collective-permute-start(f32[96,256]{1,0:T(8,128)S(1)} %add_add_fusion.2), channel_id=1, source_target_pairs={{0,16},{1,17},{2,18},{3,19},{4,20},{5,21},{6,22},{7,23},{8,24},{9,... | collective-permute-start | bytes 294920 | tf_op jit(solution)/shard_map/ppermute | solution.py:364
  94.4 7.8 %collective-permute-start.19 = (f32[96,256]{1,0:T(8,128)S(1)}, f32[96,256]{1,0:T(8,128)S(1)}, u32[]{:S(2)}, u32[]{:S(2)}) collective-permute-start(f32[96,256]{1,0:T(8,128)S(1)} %add_add_fusion.2), channel_id=1, source_target_pairs={{0,8},{1,9},{2,10},{3,11},{4,12},{5,13},{6,14},{7,15},{8,0},{9,1},... | collective-permute-start | bytes 294920 | tf_op jit(solution)/shard_map/ppermute | solution.py:364
  97.0 16.0 %collective-permute-start.9 = (bf16[16,96,128]{2,1,0:T(8,128)(2,1)S(1)}, bf16[16,96,128]{2,1,0:T(8,128)(2,1)S(1)}, u32[]{:S(2)}, u32[]{:S(2)}) collective-permute-start(bf16[16,96,128]{2,1,0:T(8,128)(2,1)S(1)} %get-tuple-element.36), channel_id=1, source_target_pairs={{0,126},{1,127},{2,0},{3,1},{4,2},{5,3},{6,4},{7,5},{8,6},{9,7},{1... | collective-permute-start | bytes 1179656 | tf_op jit(solution)/shard_map/ppermute | solution.py:359
  100.8 21.5 %collective-permute-start.10 = (bf16[16,96,128]{2,1,0:T(8,128)(2,1)S(1)}, bf16[16,96,128]{2,1,0:T(8,128)(2,1)S(1)}, u32[]{:S(2)}, u32[]{:S(2)}) collective-permute-start(bf16[16,96,128]{2,1,0:T(8,128)(2,1)S(1)} %get-tuple-element.37), channel_id=1, source_target_pairs={{0,125},{1,126},{2,127},{3,0},{4,1},{5,2},{6,3},{7,4},{8,5},{9,6},... | collective-permute-start | bytes 1179656 | tf_op jit(solution)/shard_map/ppermute | solution.py:359
  102.3 20.0 %collective-permute-start.24 = (f32[96,256]{1,0:T(8,128)S(1)}, f32[96,256]{1,0:T(8,128)S(1)}, u32[]{:S(2)}, u32[]{:S(2)}) collective-permute-start(f32[96,256]{1,0:T(8,128)S(1)} %add_add_fusion.1), channel_id=1, source_target_pairs={{0,6},{1,7},{2,4},{3,5},{4,2},{5,3},{6,0},{7,1},{8,14},{9,15},{10,... | collective-permute-start | bytes 294920 | tf_op jit(solution)/shard_map/ppermute | solution.py:364
  103.7 23.3 %collective-permute-start.23 = (f32[96,256]{1,0:T(8,128)S(1)}, f32[96,256]{1,0:T(8,128)S(1)}, u32[]{:S(2)}, u32[]{:S(2)}) collective-permute-start(f32[96,256]{1,0:T(8,128)S(1)} %add_add_fusion.1), channel_id=1, source_target_pairs={{0,4},{1,5},{2,6},{3,7},{4,0},{5,1},{6,2},{7,3},{8,12},{9,13},{10,... | collective-permute-start | bytes 294920 | tf_op jit(solution)/shard_map/ppermute | solution.py:364
  105.9 28.6 %collective-permute-start.22 = (f32[96,256]{1,0:T(8,128)S(1)}, f32[96,256]{1,0:T(8,128)S(1)}, u32[]{:S(2)}, u32[]{:S(2)}) collective-permute-start(f32[96,256]{1,0:T(8,128)S(1)} %add_add_fusion.1), channel_id=1, source_target_pairs={{0,2},{1,3},{2,0},{3,1},{4,6},{5,7},{6,4},{7,5},{8,10},{9,11},{10,... | collective-permute-start | bytes 294920 | tf_op jit(solution)/shard_map/ppermute | solution.py:364
  113.0 21.7 %collective-permute-start.11 = (bf16[16,96,128]{2,1,0:T(8,128)(2,1)S(1)}, bf16[16,96,128]{2,1,0:T(8,128)(2,1)S(1)}, u32[]{:S(2)}, u32[]{:S(2)}) collective-permute-start(bf16[16,96,128]{2,1,0:T(8,128)(2,1)S(1)} %get-tuple-element.38), channel_id=1, source_target_pairs={{0,124},{1,125},{2,126},{3,127},{4,0},{5,1},{6,2},{7,3},{8,4},{9,5... | collective-permute-start | bytes 1179656 | tf_op jit(solution)/shard_map/ppermute | solution.py:359
  122.3 18.6 %collective-permute-start.12 = (bf16[16,96,128]{2,1,0:T(8,128)(2,1)S(1)}, bf16[16,96,128]{2,1,0:T(8,128)(2,1)S(1)}, u32[]{:S(2)}, u32[]{:S(2)}) collective-permute-start(bf16[16,96,128]{2,1,0:T(8,128)(2,1)S(1)} %get-tuple-element.39), channel_id=1, source_target_pairs={{0,1},{1,2},{2,3},{3,4},{4,5},{5,6},{6,7},{7,8},{8,9},{9,10},{10,1... | collective-permute-start | bytes 1179656 | tf_op jit(solution)/shard_map/ppermute | solution.py:359
  122.3 19.7 %collective-permute-start.13 = (bf16[16,96,128]{2,1,0:T(8,128)(2,1)S(1)}, bf16[16,96,128]{2,1,0:T(8,128)(2,1)S(1)}, u32[]{:S(2)}, u32[]{:S(2)}) collective-permute-start(bf16[16,96,128]{2,1,0:T(8,128)(2,1)S(1)} %get-tuple-element.40), channel_id=1, source_target_pairs={{0,2},{1,3},{2,4},{3,5},{4,6},{5,7},{6,8},{7,9},{8,10},{9,11},{10,... | collective-permute-start | bytes 1179656 | tf_op jit(solution)/shard_map/ppermute | solution.py:359
  127.0 35.9 %collective-permute-start.14 = (bf16[16,96,128]{2,1,0:T(8,128)(2,1)S(1)}, bf16[16,96,128]{2,1,0:T(8,128)(2,1)S(1)}, u32[]{:S(2)}, u32[]{:S(2)}) collective-permute-start(bf16[16,96,128]{2,1,0:T(8,128)(2,1)S(1)} %get-tuple-element.41), channel_id=1, source_target_pairs={{0,3},{1,4},{2,5},{3,6},{4,7},{5,8},{6,9},{7,10},{8,11},{9,12},{10... | collective-permute-start | bytes 1179656 | tf_op jit(solution)/shard_map/ppermute | solution.py:359
  134.5 37.6 %collective-permute-start.15 = (bf16[16,96,128]{2,1,0:T(8,128)(2,1)S(1)}, bf16[16,96,128]{2,1,0:T(8,128)(2,1)S(1)}, u32[]{:S(2)}, u32[]{:S(2)}) collective-permute-start(bf16[16,96,128]{2,1,0:T(8,128)(2,1)S(1)} %get-tuple-element.42), channel_id=1, source_target_pairs={{0,4},{1,5},{2,6},{3,7},{4,8},{5,9},{6,10},{7,11},{8,12},{9,13},{1... | collective-permute-start | bytes 1179656 | tf_op jit(solution)/shard_map/ppermute | solution.py:359
  134.7 42.0 %collective-permute-start.25 = (f32[96,256]{1,0:T(8,128)S(1)}, f32[96,256]{1,0:T(8,128)S(1)}, u32[]{:S(2)}, u32[]{:S(2)}) collective-permute-start(f32[96,256]{1,0:T(8,128)S(1)} %add_add_fusion), channel_id=1, source_target_pairs={{0,1},{1,0},{2,3},{3,2},{4,5},{5,4},{6,7},{7,6},{8,9},{9,8},{10,11... | collective-permute-start | bytes 294920 | tf_op jit(solution)/shard_map/ppermute | solution.py:364
  (6 other events, 68.7 us)
where the time goes:
time: 178 us
  starting transfers between devices  67.6 us (38%)
  waiting for transfers between devices  63.1 us (35%)
  Pallas kernels  41.6 us (23%)
  local copies, waits for them, and re-layouts  4.78 us (3%)
    ppermute x16, waiting for transfers between devices, shift(): return lax.ppermute(array, AXIS, [(i, (i + by) % n) for i in range(n)])  54.5 us
    ppermute x16, starting transfers between devices, shift(): return lax.ppermute(array, AXIS, [(i, (i + by) % n) for i in range(n)])  54.4 us
    pallas_call x1, Pallas kernels, back_partials(): pl.pallas_call(back_body, name='back_partials', out_shape=[jax.ShapeDtype...  18.4 us
    pallas_call x1, Pallas kernels, forward(): pl.pallas_call(forward_body, name='forward', out_shape=[jax.ShapeDtypeStr...  15.4 us
    ppermute x10, starting transfers between devices, swap(): return lax.ppermute(array, AXIS, [(i, i ^ bits) for i in range(n)])  13.2 us
    ppermute x10, waiting for transfers between devices, swap(): return lax.ppermute(array, AXIS, [(i, i ^ bits) for i in range(n)])  8.59 us
    pallas_call x1, Pallas kernels, finish_adjoint(): pl.pallas_call(finish_body, name='finish_adjoint', out_shape=jax.ShapeDty...  4.57 us
  transfers between devices with their start and end apart: 26, of which 11 were waited for; matrix products, arithmetic and copies ran while one was open for 0% of the time, Pallas kernels for 14%

commit v1 on v0

v1 whole, which is shorter than its diff:
```python
import math

import jax
import jax.numpy as jnp
from jax import lax
from jax.experimental import pallas as pl
from jax.experimental.pallas import tpu as pltpu
from jax.sharding import PartitionSpec as P


AXIS = "dom"
H = 96
F = 128
T = 128
LOC = 64
CAP = 16
PEERS = 8
TILES = 256
NODES_DEV = LOC * T
CODES = LOC + PEERS * CAP
CHUNKS = 4
PER = TILES // CHUNKS
UNROLL = 32
OFFSETS = (1, 2, 3, 4, -1, -2, -3, -4)
ORDER = (3, 7, 6, 5, 4, 2, 1, 0)
HOME = (1, 0, 5, 4, 3, 2, 7, 6)
BF = jnp.bfloat16
F32 = jnp.float32


SMEM = pl.BlockSpec(memory_space=pltpu.SMEM)
VMEM = pl.BlockSpec(memory_space=pltpu.VMEM)
HBM = pl.BlockSpec(memory_space=pltpu.HBM)
LISTS = [jax.ShapeDtypeStruct((CAP, H, T), BF)] * PEERS


def params(mib):
    return pltpu.CompilerParams(vmem_limit_bytes=mib * 1024 * 1024)


def cost(gflops, mib):
    return pl.CostEstimate(
        flops=int(gflops * 10**9), transcendentals=0, bytes_accessed=mib * 2**20
    )


def hbm(array):
    return pltpu.with_memory_space_constraint(array, pltpu.HBM)


def cols(t, width=T):
    return pl.ds(pl.multiple_of(t * width, width), width)


def gather_body(send_hbm, z_hbm, *rest):
    outs = rest[:PEERS]
    send, z, sems = rest[PEERS:]
    load_z = pltpu.make_async_copy(z_hbm, z, sems.at[0])
    load_s = pltpu.make_async_copy(send_hbm, send, sems.at[1])
    load_z.start()
    load_s.start()
    load_s.wait()
    load_z.wait()
    for o in ORDER:
        for c in range(CAP):
            outs[o][c] = z[:, cols(send[0, o, c])]


def gather_lists(send_list, z_state):
    return pl.pallas_call(
        gather_body,
        name="gather_lists",
        out_shape=LISTS,
        in_specs=[HBM, HBM],
        out_specs=[VMEM] * PEERS,
        scratch_shapes=[
            pltpu.SMEM((1, PEERS, CAP), jnp.int32),
            pltpu.VMEM((H, NODES_DEV), BF),
            pltpu.SemaphoreType.DMA((2,)),
        ],
        compiler_params=params(6),
        cost_estimate=cost(1, 5),
    )(hbm(send_list), hbm(z_state))


def back_body(src, dst, z, adj, cot_hbm, w, v_hbm, *rest):
    outs = rest[:PEERS]
    acc, masked, v, back, cot, sem, v_sems = rest[PEERS:]
    load_c = pltpu.make_async_copy(cot_hbm, cot, sem.at[0])
    load_v = [
        pltpu.make_async_copy(
            v_hbm.at[pl.ds(i * PER, PER)], v.at[pl.ds(i * PER, PER)], v_sems.at[i]
        )
        for i in range(CHUNKS)
    ]
    load_c.start()
    for copy in load_v:
        copy.start()

    def clear(j, carry):
        acc[LOC + j] = jnp.zeros((H, T), F32)
        return carry

    lax.fori_loop(0, PEERS * CAP, clear, 0, unroll=4)
    wt = w[...]

    def mask(i, carry):
        at = cols(i, 4 * T)
        kept = jnp.where(z[:, at].astype(F32) > 0, adj[:, at].astype(F32), 0.0).astype(BF)
        masked[:, at] = kept
        moved = lax.dot_general(wt, kept, (((0,), (0,)), ((), ())), preferred_element_type=F32)
        moved = moved.astype(BF)
        for j in range(4):
            back[i * 4 + j] = moved[:, j * T : (j + 1) * T]
        return carry

    lax.fori_loop(0, LOC // 4, mask, 0)
    load_c.wait()

    def own(t, carry):
        acc[t] = cot[:, cols(t)].astype(F32)
        return carry

    lax.fori_loop(0, LOC, own, 0, unroll=4)

    def step(g, carry):
        first = g * UNROLL
        parts = [
            lax.dot_general(
                back[dst[0, first + u]],
                v[first + u],
                (((1,), (1,)), ((), ())),
                preferred_element_type=F32,
            )
            for u in range(UNROLL)
        ]
        for u in range(UNROLL):
            s = src[0, first + u]
            acc[s] = acc[s] + parts[u]
        return carry

    for i in range(CHUNKS):
        load_v[i].wait()
        lax.fori_loop(i * PER // UNROLL, (i + 1) * PER // UNROLL, step, 0)
    for o in range(PEERS):

        def pack(c, carry):
            outs[o][c] = acc[LOC + o * CAP + c].astype(BF)
            return carry

        lax.fori_loop(0, CAP, pack, 0, unroll=4)


def back_partials(src, dst, z_state, adjoint, cotangent, mix_weight, tile_values):
    outs = pl.pallas_call(
        back_body,
        name="back_partials",
        out_shape=LISTS
        + [
            jax.ShapeDtypeStruct((CODES, H, T), F32),
            jax.ShapeDtypeStruct((H, NODES_DEV), BF),
            jax.ShapeDtypeStruct((TILES, T, T), BF),
        ],
        in_specs=[SMEM, SMEM, VMEM, VMEM, HBM, VMEM, HBM],
        out_specs=[VMEM] * (PEERS + 3),
        scratch_shapes=[
            pltpu.VMEM((LOC, H, T), BF),
            pltpu.VMEM((H, NODES_DEV), BF),
            pltpu.SemaphoreType.DMA((1,)),
            pltpu.SemaphoreType.DMA((CHUNKS,)),
        ],
        compiler_params=params(8),
        cost_estimate=cost(4, 20),
    )(src, dst, z_state, adjoint, hbm(cotangent), mix_weight, hbm(tile_values))
    return outs[:PEERS], outs[PEERS:]


def input_body(masked, inputs, out):
    width = 8 * T

    def step(i, total):
        at = cols(i, width)
        return total + lax.dot_general(
            masked[:, at], inputs[:, at], (((1,), (1,)), ((), ())), preferred_element_type=F32
        )

    out[...] = lax.fori_loop(0, NODES_DEV // width, step, jnp.zeros((H, F), F32))


def input_product(masked, inputs):
    return pl.pallas_call(
        input_body,
        name="input_product",
        out_shape=jax.ShapeDtypeStruct((H, F), F32),
        in_specs=[VMEM, VMEM],
        out_specs=VMEM,
        compiler_params=params(12),
        cost_estimate=cost(1, 4),
    )(masked, inputs)


def forward_body(src, dst, z, m, v, grad, *rest):
    arrived = rest[:PEERS]
    out, keep, give = rest[PEERS : PEERS + 3]
    table, agg = rest[PEERS + 3 :]

    def local(t, carry):
        table[t] = z[:, cols(t)]
        agg[t] = jnp.zeros((H, T), F32)
        return carry

    lax.fori_loop(0, LOC, local, 0, unroll=4)
    for o in range(PEERS):

        def halo(c, carry):
            table[LOC + o * CAP + c] = arrived[o][c]
            return carry

        lax.fori_loop(0, CAP, halo, 0, unroll=4)

    def step(g, carry):
        first = g * UNROLL
        parts = [
            jnp.dot(table[src[0, first + u]], v[first + u], preferred_element_type=F32)
            for u in range(UNROLL)
        ]
        for u in range(UNROLL):
            d = dst[0, first + u]
            agg[d] = agg[d] + parts[u]
        return carry

    lax.fori_loop(0, TILES // UNROLL, step, 0)

    def finish(i, total):
        at = cols(i, 4 * T)
        a = jnp.concatenate([agg[i * 4 + j].astype(BF) for j in range(4)], axis=1)
        out[:, at] = a
        return total + lax.dot_general(
            m[:, at], a, (((1,), (1,)), ((), ())), preferred_element_type=F32
        )

    total = lax.fori_loop(0, LOC // 4, finish, jnp.zeros((H, H), F32))
    scale = 1.0 / math.sqrt(NODES_DEV * 128)
    inner = grad[...] * scale
    weight = jnp.concatenate([total * scale, jnp.zeros((H, F - H), F32)], axis=1)
    first = lax.rem(lax.axis_index(AXIS), 2) == 0
    keep[...] = jnp.where(first, inner, weight)
    give[...] = jnp.where(first, weight, inner)


def forward(src, dst, z_state, masked, tile_values, grad, lists):
    return pl.pallas_call(
        forward_body,
        name="forward",
        out_shape=[
            jax.ShapeDtypeStruct((H, NODES_DEV), BF),
            jax.ShapeDtypeStruct((H, F), F32),
            jax.ShapeDtypeStruct((H, F), F32),
        ],
        in_specs=[SMEM, SMEM] + [VMEM] * (4 + PEERS),
        out_specs=[VMEM] * 3,
        scratch_shapes=[pltpu.VMEM((CODES, H, T), BF), pltpu.VMEM((LOC, H, T), F32)],
        compiler_params=params(12),
        cost_estimate=cost(3, 15),
    )(src, dst, z_state, masked, tile_values, grad, *lists)


def mix_body(a, x, w, b, out):
    wt = w[...]
    bt = b[...]

    def step(i, carry):
        at = cols(i, 4 * T)
        pre = jnp.dot(wt, a[:, at], preferred_element_type=F32) + jnp.dot(
            bt, x[:, at], preferred_element_type=F32
        )
        out[:, at] = jnp.maximum(pre, 0.0).astype(BF)
        return carry

    lax.fori_loop(0, LOC // 4, step, 0)


def mixed(aggregated, inputs, mix_weight, input_weight):
    return pl.pallas_call(
        mix_body,
        name="mixed",
        out_shape=jax.ShapeDtypeStruct((H, NODES_DEV), BF),
        in_specs=[VMEM] * 4,
        out_specs=VMEM,
        compiler_params=params(12),
        cost_estimate=cost(1, 5),
    )(aggregated, inputs, mix_weight, input_weight)


def finish_body(send, given, *rest):
    lists = rest[:PEERS]
    out, acc = rest[PEERS:]
    for o in range(PEERS):
        for c in range(CAP):
            t = send[0, o, c]
            acc[t] = acc[t] + lists[o][c].astype(F32)
    for t in range(LOC):
        out[:, t * T : (t + 1) * T] = acc[t].astype(BF)


def finish_adjoint(send_list, acc, lists):
    return pl.pallas_call(
        finish_body,
        name="finish_adjoint",
        out_shape=[
            jax.ShapeDtypeStruct((H, NODES_DEV), BF),
            jax.ShapeDtypeStruct((CODES, H, T), F32),
        ],
        in_specs=[SMEM] + [VMEM] * (1 + PEERS),
        out_specs=[VMEM] * 2,
        input_output_aliases={1: 1},
        compiler_params=params(8),
        cost_estimate=cost(1, 8),
    )(send_list, acc, *lists)[0]


def ending_body(mine, theirs, weight, inner):
    first = lax.rem(lax.axis_index(AXIS), 2) == 0
    inner[...] = jnp.where(first, mine[...], theirs[...])
    weight[...] = jnp.where(first, theirs[:, :H], mine[:, :H])


def ending(mine, theirs):
    return pl.pallas_call(
        ending_body,
        name="ending",
        out_shape=[jax.ShapeDtypeStruct((H, H), F32), jax.ShapeDtypeStruct((H, F), F32)],
        in_specs=[VMEM, VMEM],
        out_specs=[VMEM] * 2,
        compiler_params=params(4),
    )(mine, theirs)


def shift(array, by):
    n = lax.axis_size(AXIS)
    return lax.ppermute(array, AXIS, [(i, (i + by) % n) for i in range(n)])


def swap(array, bits):
    n = lax.axis_size(AXIS)
    return lax.ppermute(array, AXIS, [(i, i ^ bits) for i in range(n)])


def quads(total):
    for low in (5, 3, 1):
        one, two, three = (swap(total, k << low) for k in (1, 2, 3))
        total = (total + one) + (two + three)
    return total


def exchange(lists, sign, order):
    got = [None] * PEERS
    for o in order:
        got[o] = shift(lists[o], sign * OFFSETS[o])
    return got


def per_device(
    z_state,
    inputs,
    adjoint,
    cotangent,
    mix_weight,
    input_weight,
    tile_values,
    tile_src,
    tile_dst,
    send_list,
):
    arrived = exchange(gather_lists(send_list, z_state), 1, ORDER)
    leaving, (acc, masked, held) = back_partials(
        tile_src, tile_dst, z_state, adjoint, cotangent, mix_weight, tile_values
    )
    returned = exchange(leaving, -1, HOME)
    grad = input_product(masked, inputs)
    aggregated, keep, give = forward(
        tile_src, tile_dst, z_state, masked, held, grad, arrived
    )
    total = keep + swap(give, 1)
    total = quads(total)
    fixed_next = mixed(aggregated, inputs, mix_weight, input_weight)
    adjoint_next = finish_adjoint(send_list, acc, returned)
    other = swap(total, 1)
    weight, inner = ending(total, other)
    return fixed_next, adjoint_next, weight, inner


def solution(mesh):
    dom = P(None, AXIS)
    return jax.shard_map(
        per_device,
        mesh=mesh,
        in_specs=(
            dom,
            dom,
            dom,
            dom,
            P(),
            P(),
            P(AXIS, None, None),
            P(AXIS, None),
            P(AXIS, None),
            P(AXIS, None, None),
        ),
        out_specs=(dom, dom, P(), P()),
        check_vma=False,
    )
```

time: 178 us -> 175 us (0.983)
  the two profiles are of different devices: /device:TPU:40 before, /device:TPU:33 now
where the time goes in v1:
time: 175 us
  starting transfers between devices  74.9 us (43%)
  waiting for transfers between devices  67.2 us (38%)
  Pallas kernels  31.7 us (18%)
    ppermute x16, waiting for transfers between devices, shift(): return lax.ppermute(array, AXIS, [(i, (i + by) % n) for i in range(n)])  58.6 us
    ppermute x16, starting transfers between devices, shift(): return lax.ppermute(array, AXIS, [(i, (i + by) % n) for i in range(n)])  49.5 us
    ppermute x11, starting transfers between devices, swap(): return lax.ppermute(array, AXIS, [(i, i ^ bits) for i in range(n)])  25.4 us
    pallas_call x1, Pallas kernels, back_partials(): pl.pallas_call(back_body, name='back_partials', out_shape=LISTS + [jax.Sh...  12 us
    ppermute x11, waiting for transfers between devices, swap(): return lax.ppermute(array, AXIS, [(i, i ^ bits) for i in range(n)])  8.63 us
    pallas_call x1, Pallas kernels, forward(): pl.pallas_call(forward_body, name='forward', out_shape=[jax.ShapeDtypeStr...  7.61 us
    pallas_call x1, Pallas kernels, mixed(): pl.pallas_call(mix_body, name='mixed', out_shape=jax.ShapeDtypeStruct((H,...  4.28 us
  transfers between devices with their start and end apart: 27, of which 12 were waited for; matrix products, arithmetic and copies ran while one was open for 0% of the time, Pallas kernels for 12%

profile of v1, /device:TPU:33, one launch (start us, length us, event | category | flops | bytes accessed | tf_op | source)
XLA Modules:
  0.0 174.7 jit_solution(16765491341177986325)
XLA Ops:
  0.7 2.4 %gather_lists.1 = (bf16[16,96,128]{2,1,0:T(8,128)(2,1)S(1)}, bf16[16,96,128]{2,1,0:T(8,128)(2,1)S(1)}, bf16[16,96,128]{2,1,0:T(8,128)(2,1)S(1)}, bf16[16,96,128]...) custom-call(s32[1,8,16]{2,1,0:T(8,128)} %send.1, ...), custom_call_target="tpu_custom_call" | custom-call | flops 1000000000 | bytes 5242880 | tf_op jit(solution)/shard_map/gather_lists/pallas_call | solution.py:70
  3.1 2.3 %collective-permute-start = (bf16[16,96,128]{2,1,0:T(8,128)(2,1)S(1)}, bf16[16,96,128]{2,1,0:T(8,128)(2,1)S(1)}, u32[]{:S(2)}, u32[]{:S(2)}) collective-permute-start(bf16[16,96,128]{2,1,0:T(8,128)(2,1)S(1)} %get-tuple-element.31), channel_id=1, source_target_pairs={{0,1},{1,2},{2,3},{3,4},{4,5},{5,6},{6,7},{7,8},{8,9},{9,10},{10,1... | collective-permute-start | bytes 1179656 | tf_op jit(solution)/shard_map/ppermute | solution.py:341
  5.3 1.3 collective-permute-start.1
  6.7 2.9 %collective-permute-start.3 = (bf16[16,96,128]{2,1,0:T(8,128)(2,1)S(1)}, bf16[16,96,128]{2,1,0:T(8,128)(2,1)S(1)}, u32[]{:S(2)}, u32[]{:S(2)}) collective-permute-start(bf16[16,96,128]{2,1,0:T(8,128)(2,1)S(1)} %get-tuple-element.34), channel_id=1, source_target_pairs={{0,4},{1,5},{2,6},{3,7},{4,8},{5,9},{6,10},{7,11},{8,12},{9,13},{1... | collective-permute-start | bytes 1179656 | tf_op jit(solution)/shard_map/ppermute | solution.py:341
  9.6 0.6 collective-permute-start.4
  10.2 3.4 %collective-permute-done.rest_0_ = bf16[16,96,128]{2,1,0:T(8,128)(2,1)S(1)} collective-permute-done((bf16[16,96,128]{2,1,0:T(8,128)(2,1)S(1)}, bf16[16,96,128]{2,1,0:T(8,128)(2,1)S(1)}, u32[]{:S(2)}, u32[]{:S(2)}) %collective-permute-start) | collective-permute-done | bytes 393248 | tf_op jit(solution)/shard_map/ppermute | solution.py:341
  13.6 9.0 %collective-permute-done.1.rest_1_ = bf16[16,96,128]{2,1,0:T(8,128)(2,1)S(1)} collective-permute-done((bf16[16,96,128]{2,1,0:T(8,128)(2,1)S(1)}, bf16[16,96,128]{2,1,0:T(8,128)(2,1)S(1)}, u32[]{:S(2)}, u32[]{:S(2)}) %collective-permute-start.1) | collective-permute-done | bytes 393248 | tf_op jit(solution)/shard_map/ppermute | solution.py:341
  22.6 9.6 %collective-permute-start.6 = (bf16[16,96,128]{2,1,0:T(8,128)(2,1)S(1)}, bf16[16,96,128]{2,1,0:T(8,128)(2,1)S(1)}, u32[]{:S(2)}, u32[]{:S(2)}) collective-permute-start(bf16[16,96,128]{2,1,0:T(8,128)(2,1)S(1)} %get-tuple-element.37), channel_id=1, source_target_pairs={{0,125},{1,126},{2,127},{3,0},{4,1},{5,2},{6,3},{7,4},{8,5},{9,6},... | collective-permute-start | bytes 1179656 | tf_op jit(solution)/shard_map/ppermute | solution.py:341
  32.2 14.5 %collective-permute-start.7 = (bf16[16,96,128]{2,1,0:T(8,128)(2,1)S(1)}, bf16[16,96,128]{2,1,0:T(8,128)(2,1)S(1)}, u32[]{:S(2)}, u32[]{:S(2)}) collective-permute-start(bf16[16,96,128]{2,1,0:T(8,128)(2,1)S(1)} %get-tuple-element.38), channel_id=1, source_target_pairs={{0,124},{1,125},{2,126},{3,127},{4,0},{5,1},{6,2},{7,3},{8,4},{9,5... | collective-permute-start | bytes 1179656 | tf_op jit(solution)/shard_map/ppermute | solution.py:341
  46.7 12.0 %back_partials.1 = (bf16[16,96,128]{2,1,0:T(8,128)(2,1)S(1)}, bf16[16,96,128]{2,1,0:T(8,128)(2,1)S(1)}, bf16[16,96,128]{2,1,0:T(8,128)(2,1)S(1)}, bf16[16,96,128...) custom-call(s32[1,256]{1,0:T(1,128)S(1)} %copy-done.5, ...), custom_call_target="tpu_custom_call" | custom-call | flops 4000000000 | bytes 20971520 | tf_op jit(solution)/shard_map/back_partials/pallas_call | solution.py:155
  58.7 1.8 %input_product.1.grad = f32[96,128]{1,0:T(8,128)S(1)} custom-call(bf16[96,8192]{1,0:T(8,128)(2,1)S(1)} %get-tuple-element.29.masked.m, bf16[128,8192]{1,0:T(8,128)(2,1)S(1)} %copy-done), custom_call_target="tpu_custom_call" | custom-call | flops 1000000000 | bytes 4194304 | tf_op jit(solution)/shard_map/input_product/pallas_call | solution.py:191
  60.6 2.6 %collective-permute-done.7.rest_7_ = bf16[16,96,128]{2,1,0:T(8,128)(2,1)S(1)} collective-permute-done((bf16[16,96,128]{2,1,0:T(8,128)(2,1)S(1)}, bf16[16,96,128]{2,1,0:T(8,128)(2,1)S(1)}, u32[]{:S(2)}, u32[]{:S(2)}) %collective-permute-start.7) | collective-permute-done | bytes 393248 | tf_op jit(solution)/shard_map/ppermute | solution.py:341
  63.2 7.6 %forward.1 = (bf16[96,8192]{1,0:T(8,128)(2,1)S(1)}, f32[96,128]{1,0:T(8,128)S(1)}, f32[96,128]{1,0:T(8,128)S(1)}) custom-call(s32[1,256]{1,0:T(1,128)S(1)} %copy-done.5, s32[1,256]{1,0:T(1,128)S(1)} %copy-done.6, bf16[96,8192]{1,0:T(8,128)(2,1)S(1)} %copy-done.1, bf16[96,8192]{1,0:T(8,128)(2,1)S(1)} %get-tuple-element.29.masked.m, ...), custom_call_target="tpu_custom_call" | custom-call | flops 3000000000 | bytes 15728640 | tf_op jit(solution)/shard_map/forward/pallas_call | solution.py:252
  70.9 1.2 collective-permute-done.16
  72.1 3.1 %collective-permute-start.19 = (f32[96,128]{1,0:T(8,128)S(1)}, f32[96,128]{1,0:T(8,128)S(1)}, u32[]{:S(2)}, u32[]{:S(2)}) collective-permute-start(f32[96,128]{1,0:T(8,128)S(1)} %add.30), channel_id=1, source_target_pairs={{0,96},{1,97},{2,98},{3,99},{4,100},{5,101},{6,102},{7,103},{8,104... | collective-permute-start | bytes 147464 | tf_op jit(solution)/shard_map/ppermute | solution.py:346
  75.9 0.6 collective-permute-start.8
  76.6 0.7 collective-permute-done.19
  77.3 4.9 %collective-permute-start.10 = (bf16[16,96,128]{2,1,0:T(8,128)(2,1)S(1)}, bf16[16,96,128]{2,1,0:T(8,128)(2,1)S(1)}, u32[]{:S(2)}, u32[]{:S(2)}) collective-permute-start(bf16[16,96,128]{2,1,0:T(8,128)(2,1)S(1)} %get-tuple-element.43), channel_id=1, source_target_pairs={{0,125},{1,126},{2,127},{3,0},{4,1},{5,2},{6,3},{7,4},{8,5},{9,6},... | collective-permute-start | bytes 1179656 | tf_op jit(solution)/shard_map/ppermute | solution.py:341
  83.0 3.4 %collective-permute-done.22 = f32[96,128]{1,0:T(8,128)S(1)} collective-permute-done((f32[96,128]{1,0:T(8,128)S(1)}, f32[96,128]{1,0:T(8,128)S(1)}, u32[]{:S(2)}, u32[]{:S(2)}) %collective-permute-start.22) | collective-permute-done | bytes 49184 | tf_op jit(solution)/shard_map/ppermute | solution.py:346
  86.4 0.5 collective-permute-done.21
  87.0 2.7 %collective-permute-done.20 = f32[96,128]{1,0:T(8,128)S(1)} collective-permute-done((f32[96,128]{1,0:T(8,128)S(1)}, f32[96,128]{1,0:T(8,128)S(1)}, u32[]{:S(2)}, u32[]{:S(2)}) %collective-permute-start.20) | collective-permute-done | bytes 49184 | tf_op jit(solution)/shard_map/ppermute | solution.py:346
  89.7 1.9 %collective-permute-start.25 = (f32[96,128]{1,0:T(8,128)S(1)}, f32[96,128]{1,0:T(8,128)S(1)}, u32[]{:S(2)}, u32[]{:S(2)}) collective-permute-start(f32[96,128]{1,0:T(8,128)S(1)} %add_add_fusion.1), channel_id=1, source_target_pairs={{0,6},{1,7},{2,4},{3,5},{4,2},{5,3},{6,0},{7,1},{8,14},{9,15},{10,... | collective-permute-start | bytes 147464 | tf_op jit(solution)/shard_map/ppermute | solution.py:346
  91.6 18.3 %collective-permute-start.24 = (f32[96,128]{1,0:T(8,128)S(1)}, f32[96,128]{1,0:T(8,128)S(1)}, u32[]{:S(2)}, u32[]{:S(2)}) collective-permute-start(f32[96,128]{1,0:T(8,128)S(1)} %add_add_fusion.1), channel_id=1, source_target_pairs={{0,4},{1,5},{2,6},{3,7},{4,0},{5,1},{6,2},{7,3},{8,12},{9,13},{10,... | collective-permute-start | bytes 147464 | tf_op jit(solution)/shard_map/ppermute | solution.py:346
  109.9 4.0 %collective-permute-start.11 = (bf16[16,96,128]{2,1,0:T(8,128)(2,1)S(1)}, bf16[16,96,128]{2,1,0:T(8,128)(2,1)S(1)}, u32[]{:S(2)}, u32[]{:S(2)}) collective-permute-start(bf16[16,96,128]{2,1,0:T(8,128)(2,1)S(1)} %get-tuple-element.44), channel_id=1, source_target_pairs={{0,124},{1,125},{2,126},{3,127},{4,0},{5,1},{6,2},{7,3},{8,4},{9,5... | collective-permute-start | bytes 1179656 | tf_op jit(solution)/shard_map/ppermute | solution.py:341
  113.8 5.6 %collective-permute-start.12 = (bf16[16,96,128]{2,1,0:T(8,128)(2,1)S(1)}, bf16[16,96,128]{2,1,0:T(8,128)(2,1)S(1)}, u32[]{:S(2)}, u32[]{:S(2)}) collective-permute-start(bf16[16,96,128]{2,1,0:T(8,128)(2,1)S(1)} %get-tuple-element.45), channel_id=1, source_target_pairs={{0,1},{1,2},{2,3},{3,4},{4,5},{5,6},{6,7},{7,8},{8,9},{9,10},{10,1... | collective-permute-start | bytes 1179656 | tf_op jit(solution)/shard_map/ppermute | solution.py:341
  119.9 2.8 %collective-permute-start.14 = (bf16[16,96,128]{2,1,0:T(8,128)(2,1)S(1)}, bf16[16,96,128]{2,1,0:T(8,128)(2,1)S(1)}, u32[]{:S(2)}, u32[]{:S(2)}) collective-permute-start(bf16[16,96,128]{2,1,0:T(8,128)(2,1)S(1)} %get-tuple-element.47), channel_id=1, source_target_pairs={{0,3},{1,4},{2,5},{3,6},{4,7},{5,8},{6,9},{7,10},{8,11},{9,12},{10... | collective-permute-start | bytes 1179656 | tf_op jit(solution)/shard_map/ppermute | solution.py:341
  122.7 4.3 %mixed.1 = bf16[96,8192]{1,0:T(8,128)(2,1)} custom-call(bf16[96,8192]{1,0:T(8,128)(2,1)S(1)} %get-tuple-element.39.a, bf16[128,8192]{1,0:T(8,128)(2,1)S(1)} %copy-done, bf16[96,96]{1,0:T(8,128)(2,1)S(1)} %copy-done.2, bf16[96,128]{1,0:T(8,128)(2,1)S(1)} %copy-done.3), custom_call_target="tpu_custom_call" | custom-call | flops 1000000000 | bytes 5242880 | tf_op jit(solution)/shard_map/mixed/pallas_call | solution.py:284
  127.5 4.9 %collective-permute-done.12.rest_4_ = bf16[16,96,128]{2,1,0:T(8,128)(2,1)S(1)} collective-permute-done((bf16[16,96,128]{2,1,0:T(8,128)(2,1)S(1)}, bf16[16,96,128]{2,1,0:T(8,128)(2,1)S(1)}, u32[]{:S(2)}, u32[]{:S(2)}) %collective-permute-start.12) | collective-permute-done | bytes 393248 | tf_op jit(solution)/shard_map/ppermute | solution.py:341
  132.5 9.3 %collective-permute-done.13.rest_5_ = bf16[16,96,128]{2,1,0:T(8,128)(2,1)S(1)} collective-permute-done((bf16[16,96,128]{2,1,0:T(8,128)(2,1)S(1)}, bf16[16,96,128]{2,1,0:T(8,128)(2,1)S(1)}, u32[]{:S(2)}, u32[]{:S(2)}) %collective-permute-start.13) | collective-permute-done | bytes 393248 | tf_op jit(solution)/shard_map/ppermute | solution.py:341
  141.9 29.2 %collective-permute-done.15.rest_7_ = bf16[16,96,128]{2,1,0:T(8,128)(2,1)S(1)} collective-permute-done((bf16[16,96,128]{2,1,0:T(8,128)(2,1)S(1)}, bf16[16,96,128]{2,1,0:T(8,128)(2,1)S(1)}, u32[]{:S(2)}, u32[]{:S(2)}) %collective-permute-start.15) | collective-permute-done | bytes 393248 | tf_op jit(solution)/shard_map/ppermute | solution.py:341
  171.1 2.9 %finish_adjoint.1 = (bf16[96,8192]{1,0:T(8,128)(2,1)}, f32[192,96,128]{2,1,0:T(8,128)S(1)}) custom-call(s32[1,8,16]{2,1,0:T(8,128)S(1)} %copy-done.4, f32[192,96,128]{2,1,0:T(8,128)S(1)} %get-tuple-element.40.given, bf16[16,96,128]{2,1,0:T(8,128)(2,1)S(1)} %collective-permute-done.8.rest_0_, ...), custom_call_target="tpu_custom_call", output_to_operand_aliasing={{1}: (1, {})} | custom-call | flops 1000000000 | bytes 8388608 | tf_op jit(solution)/shard_map/finish_adjoint/pallas_call | solution.py:307
  174.0 0.6 ending.1
  (49 shorter events, 2.7 us)
Async XLA Ops:
  0.6 46.0 %copy-start.1 = (bf16[96,8192]{1,0:T(8,128)(2,1)S(1)}, bf16[96,8192]{1,0:T(8,128)(2,1)}, u32[]{:S(2)}) copy-start(bf16[96,8192]{1,0:T(8,128)(2,1)} %z.3) | copy-start | bytes 4718596
  0.6 46.0 %copy-start.6 = (s32[1,256]{1,0:T(1,128)S(1)}, s32[1,256]{1,0:T(1,128)}, u32[]{:S(2)}) copy-start(s32[1,256]{1,0:T(1,128)} %dst.3) | copy-start | bytes 3076
  0.7 46.0 %copy-start.5 = (s32[1,256]{1,0:T(1,128)S(1)}, s32[1,256]{1,0:T(1,128)}, u32[]{:S(2)}) copy-start(s32[1,256]{1,0:T(1,128)} %src.3) | copy-start | bytes 3076
  3.1 10.5 %collective-permute-start = (bf16[16,96,128]{2,1,0:T(8,128)(2,1)S(1)}, bf16[16,96,128]{2,1,0:T(8,128)(2,1)S(1)}, u32[]{:S(2)}, u32[]{:S(2)}) collective-permute-start(bf16[16,96,128]{2,1,0:T(8,128)(2,1)S(1)} %get-tuple-element.31), channel_id=1, source_target_pairs={{0,1},{1,2},{2,3},{3,4},{4,5},{5,6},{6,7},{7,8},{8,9},{9,10},{10,1... | collective-permute-start | bytes 1179656 | tf_op jit(solution)/shard_map/ppermute | solution.py:341
  5.3 17.3 %collective-permute-start.1 = (bf16[16,96,128]{2,1,0:T(8,128)(2,1)S(1)}, bf16[16,96,128]{2,1,0:T(8,128)(2,1)S(1)}, u32[]{:S(2)}, u32[]{:S(2)}) collective-permute-start(bf16[16,96,128]{2,1,0:T(8,128)(2,1)S(1)} %get-tuple-element.32), channel_id=1, source_target_pairs={{0,2},{1,3},{2,4},{3,5},{4,6},{5,7},{6,8},{7,9},{8,10},{9,11},{10,... | collective-permute-start | bytes 1179656 | tf_op jit(solution)/shard_map/ppermute | solution.py:341
  6.7 25.5 %collective-permute-start.2 = (bf16[16,96,128]{2,1,0:T(8,128)(2,1)S(1)}, bf16[16,96,128]{2,1,0:T(8,128)(2,1)S(1)}, u32[]{:S(2)}, u32[]{:S(2)}) collective-permute-start(bf16[16,96,128]{2,1,0:T(8,128)(2,1)S(1)} %get-tuple-element.33), channel_id=1, source_target_pairs={{0,3},{1,4},{2,5},{3,6},{4,7},{5,8},{6,9},{7,10},{8,11},{9,12},{10... | collective-permute-start | bytes 1179656 | tf_op jit(solution)/shard_map/ppermute | solution.py:341
  6.7 53.8 %collective-permute-start.3 = (bf16[16,96,128]{2,1,0:T(8,128)(2,1)S(1)}, bf16[16,96,128]{2,1,0:T(8,128)(2,1)S(1)}, u32[]{:S(2)}, u32[]{:S(2)}) collective-permute-start(bf16[16,96,128]{2,1,0:T(8,128)(2,1)S(1)} %get-tuple-element.34), channel_id=1, source_target_pairs={{0,4},{1,5},{2,6},{3,7},{4,8},{5,9},{6,10},{7,11},{8,12},{9,13},{1... | collective-permute-start | bytes 1179656 | tf_op jit(solution)/shard_map/ppermute | solution.py:341
  9.6 50.9 %collective-permute-start.4 = (bf16[16,96,128]{2,1,0:T(8,128)(2,1)S(1)}, bf16[16,96,128]{2,1,0:T(8,128)(2,1)S(1)}, u32[]{:S(2)}, u32[]{:S(2)}) collective-permute-start(bf16[16,96,128]{2,1,0:T(8,128)(2,1)S(1)} %get-tuple-element.35), channel_id=1, source_target_pairs={{0,127},{1,0},{2,1},{3,2},{4,3},{5,4},{6,5},{7,6},{8,7},{9,8},{10,... | collective-permute-start | bytes 1179656 | tf_op jit(solution)/shard_map/ppermute | solution.py:341
  13.6 46.9 %collective-permute-start.5 = (bf16[16,96,128]{2,1,0:T(8,128)(2,1)S(1)}, bf16[16,96,128]{2,1,0:T(8,128)(2,1)S(1)}, u32[]{:S(2)}, u32[]{:S(2)}) collective-permute-start(bf16[16,96,128]{2,1,0:T(8,128)(2,1)S(1)} %get-tuple-element.36), channel_id=1, source_target_pairs={{0,126},{1,127},{2,0},{3,1},{4,2},{5,3},{6,4},{7,5},{8,6},{9,7},{1... | collective-permute-start | bytes 1179656 | tf_op jit(solution)/shard_map/ppermute | solution.py:341
  22.6 37.9 %collective-permute-start.6 = (bf16[16,96,128]{2,1,0:T(8,128)(2,1)S(1)}, bf16[16,96,128]{2,1,0:T(8,128)(2,1)S(1)}, u32[]{:S(2)}, u32[]{:S(2)}) collective-permute-start(bf16[16,96,128]{2,1,0:T(8,128)(2,1)S(1)} %get-tuple-element.37), channel_id=1, source_target_pairs={{0,125},{1,126},{2,127},{3,0},{4,1},{5,2},{6,3},{7,4},{8,5},{9,6},... | collective-permute-start | bytes 1179656 | tf_op jit(solution)/shard_map/ppermute | solution.py:341
  32.2 31.0 %collective-permute-start.7 = (bf16[16,96,128]{2,1,0:T(8,128)(2,1)S(1)}, bf16[16,96,128]{2,1,0:T(8,128)(2,1)S(1)}, u32[]{:S(2)}, u32[]{:S(2)}) collective-permute-start(bf16[16,96,128]{2,1,0:T(8,128)(2,1)S(1)} %get-tuple-element.38), channel_id=1, source_target_pairs={{0,124},{1,125},{2,126},{3,127},{4,0},{5,1},{6,2},{7,3},{8,4},{9,5... | collective-permute-start | bytes 1179656 | tf_op jit(solution)/shard_map/ppermute | solution.py:341
  63.2 59.5 %copy-start.3 = (bf16[96,128]{1,0:T(8,128)(2,1)S(1)}, bf16[96,128]{1,0:T(8,128)(2,1)}, u32[]{:S(2)}) copy-start(bf16[96,128]{1,0:T(8,128)(2,1)} %b.1) | copy-start | bytes 73732
  70.8 1.3 collective-permute-start.16
  72.1 5.2 %collective-permute-start.19 = (f32[96,128]{1,0:T(8,128)S(1)}, f32[96,128]{1,0:T(8,128)S(1)}, u32[]{:S(2)}, u32[]{:S(2)}) collective-permute-start(f32[96,128]{1,0:T(8,128)S(1)} %add.30), channel_id=1, source_target_pairs={{0,96},{1,97},{2,98},{3,99},{4,100},{5,101},{6,102},{7,103},{8,104... | collective-permute-start | bytes 147464 | tf_op jit(solution)/shard_map/ppermute | solution.py:346
  75.3 6.9 %collective-permute-start.18 = (f32[96,128]{1,0:T(8,128)S(1)}, f32[96,128]{1,0:T(8,128)S(1)}, u32[]{:S(2)}, u32[]{:S(2)}) collective-permute-start(f32[96,128]{1,0:T(8,128)S(1)} %add.30), channel_id=1, source_target_pairs={{0,64},{1,65},{2,66},{3,67},{4,68},{5,69},{6,70},{7,71},{8,72},{9,... | collective-permute-start | bytes 147464 | tf_op jit(solution)/shard_map/ppermute | solution.py:346
  75.7 6.5 %collective-permute-start.17 = (f32[96,128]{1,0:T(8,128)S(1)}, f32[96,128]{1,0:T(8,128)S(1)}, u32[]{:S(2)}, u32[]{:S(2)}) collective-permute-start(f32[96,128]{1,0:T(8,128)S(1)} %add.30), channel_id=1, source_target_pairs={{0,32},{1,33},{2,34},{3,35},{4,36},{5,37},{6,38},{7,39},{8,40},{9,... | collective-permute-start | bytes 147464 | tf_op jit(solution)/shard_map/ppermute | solution.py:346
  75.9 33.9 %collective-permute-start.8 = (bf16[16,96,128]{2,1,0:T(8,128)(2,1)S(1)}, bf16[16,96,128]{2,1,0:T(8,128)(2,1)S(1)}, u32[]{:S(2)}, u32[]{:S(2)}) collective-permute-start(bf16[16,96,128]{2,1,0:T(8,128)(2,1)S(1)} %get-tuple-element.41), channel_id=1, source_target_pairs={{0,127},{1,0},{2,1},{3,2},{4,3},{5,4},{6,5},{7,6},{8,7},{9,8},{10,... | collective-permute-start | bytes 1179656 | tf_op jit(solution)/shard_map/ppermute | solution.py:341
  76.6 33.3 %collective-permute-start.9 = (bf16[16,96,128]{2,1,0:T(8,128)(2,1)S(1)}, bf16[16,96,128]{2,1,0:T(8,128)(2,1)S(1)}, u32[]{:S(2)}, u32[]{:S(2)}) collective-permute-start(bf16[16,96,128]{2,1,0:T(8,128)(2,1)S(1)} %get-tuple-element.42), channel_id=1, source_target_pairs={{0,126},{1,127},{2,0},{3,1},{4,2},{5,3},{6,4},{7,5},{8,6},{9,7},{1... | collective-permute-start | bytes 1179656 | tf_op jit(solution)/shard_map/ppermute | solution.py:341
  77.3 36.5 %collective-permute-start.10 = (bf16[16,96,128]{2,1,0:T(8,128)(2,1)S(1)}, bf16[16,96,128]{2,1,0:T(8,128)(2,1)S(1)}, u32[]{:S(2)}, u32[]{:S(2)}) collective-permute-start(bf16[16,96,128]{2,1,0:T(8,128)(2,1)S(1)} %get-tuple-element.43), channel_id=1, source_target_pairs={{0,125},{1,126},{2,127},{3,0},{4,1},{5,2},{6,3},{7,4},{8,5},{9,6},... | collective-permute-start | bytes 1179656 | tf_op jit(solution)/shard_map/ppermute | solution.py:341
  82.2 4.2 %collective-permute-start.22 = (f32[96,128]{1,0:T(8,128)S(1)}, f32[96,128]{1,0:T(8,128)S(1)}, u32[]{:S(2)}, u32[]{:S(2)}) collective-permute-start(f32[96,128]{1,0:T(8,128)S(1)} %add_add_fusion.2), channel_id=1, source_target_pairs={{0,24},{1,25},{2,26},{3,27},{4,28},{5,29},{6,30},{7,31},{8,16},{9,... | collective-permute-start | bytes 147464 | tf_op jit(solution)/shard_map/ppermute | solution.py:346
  82.5 4.4 %collective-permute-start.21 = (f32[96,128]{1,0:T(8,128)S(1)}, f32[96,128]{1,0:T(8,128)S(1)}, u32[]{:S(2)}, u32[]{:S(2)}) collective-permute-start(f32[96,128]{1,0:T(8,128)S(1)} %add_add_fusion.2), channel_id=1, source_target_pairs={{0,16},{1,17},{2,18},{3,19},{4,20},{5,21},{6,22},{7,23},{8,24},{9,... | collective-permute-start | bytes 147464 | tf_op jit(solution)/shard_map/ppermute | solution.py:346
  86.4 3.2 %collective-permute-start.20 = (f32[96,128]{1,0:T(8,128)S(1)}, f32[96,128]{1,0:T(8,128)S(1)}, u32[]{:S(2)}, u32[]{:S(2)}) collective-permute-start(f32[96,128]{1,0:T(8,128)S(1)} %add_add_fusion.2), channel_id=1, source_target_pairs={{0,8},{1,9},{2,10},{3,11},{4,12},{5,13},{6,14},{7,15},{8,0},{9,1},... | collective-permute-start | bytes 147464 | tf_op jit(solution)/shard_map/ppermute | solution.py:346
  89.7 29.8 %collective-permute-start.25 = (f32[96,128]{1,0:T(8,128)S(1)}, f32[96,128]{1,0:T(8,128)S(1)}, u32[]{:S(2)}, u32[]{:S(2)}) collective-permute-start(f32[96,128]{1,0:T(8,128)S(1)} %add_add_fusion.1), channel_id=1, source_target_pairs={{0,6},{1,7},{2,4},{3,5},{4,2},{5,3},{6,0},{7,1},{8,14},{9,15},{10,... | collective-permute-start | bytes 147464 | tf_op jit(solution)/shard_map/ppermute | solution.py:346
  91.6 28.3 %collective-permute-start.24 = (f32[96,128]{1,0:T(8,128)S(1)}, f32[96,128]{1,0:T(8,128)S(1)}, u32[]{:S(2)}, u32[]{:S(2)}) collective-permute-start(f32[96,128]{1,0:T(8,128)S(1)} %add_add_fusion.1), channel_id=1, source_target_pairs={{0,4},{1,5},{2,6},{3,7},{4,0},{5,1},{6,2},{7,3},{8,12},{9,13},{10,... | collective-permute-start | bytes 147464 | tf_op jit(solution)/shard_map/ppermute | solution.py:346
  109.9 12.8 %collective-permute-start.23 = (f32[96,128]{1,0:T(8,128)S(1)}, f32[96,128]{1,0:T(8,128)S(1)}, u32[]{:S(2)}, u32[]{:S(2)}) collective-permute-start(f32[96,128]{1,0:T(8,128)S(1)} %add_add_fusion.1), channel_id=1, source_target_pairs={{0,2},{1,3},{2,0},{3,1},{4,6},{5,7},{6,4},{7,5},{8,10},{9,11},{10,... | collective-permute-start | bytes 147464 | tf_op jit(solution)/shard_map/ppermute | solution.py:346
  109.9 17.1 %collective-permute-start.11 = (bf16[16,96,128]{2,1,0:T(8,128)(2,1)S(1)}, bf16[16,96,128]{2,1,0:T(8,128)(2,1)S(1)}, u32[]{:S(2)}, u32[]{:S(2)}) collective-permute-start(bf16[16,96,128]{2,1,0:T(8,128)(2,1)S(1)} %get-tuple-element.44), channel_id=1, source_target_pairs={{0,124},{1,125},{2,126},{3,127},{4,0},{5,1},{6,2},{7,3},{8,4},{9,5... | collective-permute-start | bytes 1179656 | tf_op jit(solution)/shard_map/ppermute | solution.py:341
  113.8 18.6 %collective-permute-start.12 = (bf16[16,96,128]{2,1,0:T(8,128)(2,1)S(1)}, bf16[16,96,128]{2,1,0:T(8,128)(2,1)S(1)}, u32[]{:S(2)}, u32[]{:S(2)}) collective-permute-start(bf16[16,96,128]{2,1,0:T(8,128)(2,1)S(1)} %get-tuple-element.45), channel_id=1, source_target_pairs={{0,1},{1,2},{2,3},{3,4},{4,5},{5,6},{6,7},{7,8},{8,9},{9,10},{10,1... | collective-permute-start | bytes 1179656 | tf_op jit(solution)/shard_map/ppermute | solution.py:341
  119.5 22.3 %collective-permute-start.13 = (bf16[16,96,128]{2,1,0:T(8,128)(2,1)S(1)}, bf16[16,96,128]{2,1,0:T(8,128)(2,1)S(1)}, u32[]{:S(2)}, u32[]{:S(2)}) collective-permute-start(bf16[16,96,128]{2,1,0:T(8,128)(2,1)S(1)} %get-tuple-element.46), channel_id=1, source_target_pairs={{0,2},{1,3},{2,4},{3,5},{4,6},{5,7},{6,8},{7,9},{8,10},{9,11},{10,... | collective-permute-start | bytes 1179656 | tf_op jit(solution)/shard_map/ppermute | solution.py:341
  119.9 22.0 %collective-permute-start.14 = (bf16[16,96,128]{2,1,0:T(8,128)(2,1)S(1)}, bf16[16,96,128]{2,1,0:T(8,128)(2,1)S(1)}, u32[]{:S(2)}, u32[]{:S(2)}) collective-permute-start(bf16[16,96,128]{2,1,0:T(8,128)(2,1)S(1)} %get-tuple-element.47), channel_id=1, source_target_pairs={{0,3},{1,4},{2,5},{3,6},{4,7},{5,8},{6,9},{7,10},{8,11},{9,12},{10... | collective-permute-start | bytes 1179656 | tf_op jit(solution)/shard_map/ppermute | solution.py:341
  122.7 48.4 %collective-permute-start.15 = (bf16[16,96,128]{2,1,0:T(8,128)(2,1)S(1)}, bf16[16,96,128]{2,1,0:T(8,128)(2,1)S(1)}, u32[]{:S(2)}, u32[]{:S(2)}) collective-permute-start(bf16[16,96,128]{2,1,0:T(8,128)(2,1)S(1)} %get-tuple-element.48), channel_id=1, source_target_pairs={{0,4},{1,5},{2,6},{3,7},{4,8},{5,9},{6,10},{7,11},{8,12},{9,13},{1... | collective-permute-start | bytes 1179656 | tf_op jit(solution)/shard_map/ppermute | solution.py:341
  122.7 48.4 %copy-start.4 = (s32[1,8,16]{2,1,0:T(8,128)S(1)}, s32[1,8,16]{2,1,0:T(8,128)}, u32[]{:S(2)}) copy-start(s32[1,8,16]{2,1,0:T(8,128)} %send.1) | copy-start | bytes 1540
  127.0 47.0 %collective-permute-start.26 = (f32[96,128]{1,0:T(8,128)S(1)}, f32[96,128]{1,0:T(8,128)S(1)}, u32[]{:S(2)}, u32[]{:S(2)}) collective-permute-start(f32[96,128]{1,0:T(8,128)S(1)} %add_add_fusion.mine), channel_id=1, source_target_pairs={{0,1},{1,0},{2,3},{3,2},{4,5},{5,4},{6,7},{7,6},{8,9},{9,8},{10,11... | collective-permute-start | bytes 147464 | tf_op jit(solution)/shard_map/ppermute | solution.py:346
  (3 other events, 118.5 us)
